TPU v7x, 32 devices: a whole 2x2x4 slice. The times are simulated.
32 devices in a mesh: groups: 2 (over x), ctx: 16 (over z, y, core).
Axes of the slice: x: 2, y: 2, z: 4, core: 2. Of those that a mesh axis runs over, the one named last changes fastest.
Arguments:
- queries: bfloat16 [512, 128, 576], P(('groups', 'ctx')), parts along dimension 0, may hold values from -4 to 4
- latent_cache: bfloat16 [32768, 576], P(('groups', 'ctx')), parts along dimension 0, may hold values from -4 to 4
- block_picks: int32 [32, 32], P(('groups', 'ctx')), parts along dimension 0, may hold values from 0 to 255, as said below
- lengths: int32 [512], P(('groups', 'ctx')), parts along dimension 0, may hold values from 8192 to 16384
Outputs:
- latent_out: bfloat16 [512, 128, 512], P(('groups', 'ctx')), parts along dimension 0
There are 2 independent parts, one for each index of `groups`. A program takes and returns all parts, laid end to end along the dimension named above; each array names one. Nothing has to cross between parts.
Inputs may be any that keep to these rules, and one draw needn't show every extreme that they name: `block_picks`: each row names 32 different blocks. At most 4 of a row's blocks lie in one owner's range of 16 consecutive blocks, and every row reaches this with its first 4 entries, which lie in the first half of the context. Over all rows together at most 8 different blocks of one owner's range are named, and some owner reaches this.
All inputs are finite; a program needn't handle non-finite values.
Results may differ from a plain program's by a relative error of at most 0.0035.
Values may be sent and summed in bfloat16 or wider, within the bound.
No kernel may reach another device: no remote copies, remote signals or barrier semaphores. Data moves between devices by JAX's collectives and lax.ppermute only.
A program may use at most 128 MiB of HBM per device.

v0:
```python
import jax
import jax.numpy as jnp
from jax import lax
from jax.sharding import PartitionSpec as P

LAT = 512
BLOCK = 64
TOPK = 32
SOFTMAX_SCALE = 192.0 ** (-0.5)


def attend(query_rows, key_rows, positions, row_lengths):
    total_rows = query_rows.shape[0]
    step_rows = 512
    block_count = total_rows // step_rows
    latent = key_rows[:, :LAT]

    def per_block(inputs):
        block_queries, block_lengths = inputs
        block_ratings = (
            lax.dot_general(
                block_queries,
                key_rows,
                (((1,), (1,)), ((), ())),
                preferred_element_type=jnp.float32,
            )
            * SOFTMAX_SCALE
        )
        visible = positions[None, :] < block_lengths[:, None]
        row_max = jnp.max(jnp.where(visible, block_ratings, -jnp.inf), axis=1, keepdims=True)
        exponent = jnp.where(visible, jnp.exp(block_ratings - row_max), 0.0)
        normaliser = jnp.sum(exponent, axis=1, keepdims=True)
        weights = exponent.astype(jnp.bfloat16)
        result = jnp.dot(weights, latent, preferred_element_type=jnp.float32) / normaliser
        return result.astype(jnp.bfloat16)

    outputs = lax.map(
        per_block,
        (
            query_rows.reshape(block_count, step_rows, query_rows.shape[1]),
            row_lengths.reshape(block_count, step_rows),
        ),
    )
    return outputs.reshape(total_rows, LAT)


def shards(queries, latent_cache, block_picks, lengths):
    ctx_count = lax.axis_size("ctx")
    myself = lax.axis_index("ctx")
    feature = latent_cache.shape[1]
    owned = latent_cache.shape[0] // BLOCK
    capacity = max(1, 2 * TOPK // ctx_count)
    block_rows = latent_cache.reshape(owned, BLOCK * feature)
    own_picks = block_picks[0]
    owners = own_picks // owned
    union_size = 2 * capacity
    all_picks = lax.all_gather(block_picks, "ctx", axis=0, tiled=True)
    selected_flag = (
        jnp.zeros((ctx_count * owned,), jnp.int32)
        .at[all_picks.reshape(-1)]
        .set(1)
        .reshape(ctx_count, owned)
    )
    packed_at = jnp.cumsum(selected_flag, axis=1) - 1
    own_flag = lax.dynamic_index_in_dim(selected_flag, myself, 0, keepdims=False)
    own_packed = lax.dynamic_index_in_dim(packed_at, myself, 0, keepdims=False)
    slot_ids = jnp.arange(union_size, dtype=jnp.int32)
    matches = (own_packed[None, :] == slot_ids[:, None]) & (own_flag[None, :] == 1)
    source = jnp.sum(
        matches.astype(jnp.int32) * jnp.arange(owned, dtype=jnp.int32)[None, :], axis=1
    )
    candidates = jnp.take(block_rows, source, axis=0)
    target = owners * union_size + jnp.take(packed_at.reshape(-1), own_picks)
    portion = lax.all_gather(candidates, "ctx", axis=0, tiled=True)
    indices = jnp.arange(portion.shape[0], dtype=jnp.int32)
    pick_one = (target[:, None] == indices[None, :]).astype(jnp.bfloat16)
    chosen = jnp.dot(pick_one, portion, preferred_element_type=jnp.float32).astype(jnp.bfloat16)
    key_rows = chosen.reshape(TOPK * BLOCK, feature)
    within = jnp.arange(BLOCK, dtype=jnp.int32)
    positions = (own_picks[:, None] * BLOCK + within[None, :]).reshape(-1)
    head_count = queries.shape[1]
    query_rows = queries.reshape(queries.shape[0] * head_count, feature)
    row_lengths = jnp.repeat(lengths, head_count)
    result = attend(query_rows, key_rows, positions, row_lengths)
    return result.reshape(queries.shape[0], head_count, LAT)


def solution(mesh):
    placed = (
        P(("groups", "ctx"), None, None),
        P(("groups", "ctx"), None),
        P(("groups", "ctx"), None),
        P(("groups", "ctx")),
    )
    return jax.shard_map(
        shards,
        mesh=mesh,
        in_specs=placed,
        out_specs=P(("groups", "ctx"), None, None),
        check_vma=False,
    )
```

profile of v0, /device:TPU:0, one launch (start us, length us, event | category | flops | bytes accessed | tf_op | source)
XLA Modules:
  0.0 166.6 jit_solution(2164973816998494499)
XLA Ops:
  6.5 23.3 %all-gather = s32[16,1,32]{2,1,0:T(1,128)S(1)} all-gather(s32[1,1,32]{2,1,0:T(1,128)} %bitcast.62), channel_id=1, replica_groups=mesh['groups'=2,'ctx'=16] {'ctx'}, dimensions={0}, use_global_device_ids=true | all-gather | bytes 2176 | tf_op jit(solution)/shard_map/all_gather | solution.py:57
  31.1 2.4 %scatter_custom_fusion = s32[256]{0:T(256)S(1)} fusion(s32[512]{0:T(512)S(1)} %bitcast.61, s32[512]{0:T(512)S(1)} %broadcast.154, s32[]{:T(128)} %copy.24), kind=kCustom, calls=%fused_computation.56 | custom fusion | bytes 1028 | tf_op jit(solution)/shard_map/scatter | solution.py:61
  34.0 1.7 %copy.12 = bf16[1024,576]{1,0:T(8,128)(2,1)S(1)} copy(bf16[1024,576]{0,1:T(8,128)(2,1)} %param.7) | data formatting | bytes 2359296 | tf_op args[1]
  35.7 1.6 reshape.151
  37.3 1.8 %gather_fusion.1 = bf16[8,36864]{1,0:T(8,128)(2,1)} fusion(bf16[16,36864]{1,0:T(8,128)(2,1)S(1)} %reshape.151, s32[1024]{0:T(1024)S(1)} %pad_clamp_fusion), kind=kCustom, calls=%fused_computation.1 | custom fusion | bytes 1179680 | tf_op jit(solution)/shard_map/jit(_take)/gather | solution.py:72
  39.1 2.0 %broadcast_select_fusion = bf16[8,36864]{1,0:T(8,128)(2,1)} fusion(bf16[8,36864]{1,0:T(8,128)(2,1)} %gather_fusion.1, pred[8]{0:T(512)(128)(4,1)S(1)} %compare_and_fusion), kind=kLoop, calls=%fused_computation.27 | loop fusion | flops 294912 | bytes 1179656 | tf_op jit(solution)/shard_map/jit(_take)/select_n | solution.py:72
  41.2 2.6 %copy.11 = bf16[16,128,576]{2,1,0:T(8,128)(2,1)} copy(bf16[16,128,576]{1,2,0:T(8,128)(2,1)S(1)} %copy-done) | data formatting | bytes 4718592 | tf_op args[0]
  44.7 74.8 %all-gather.3.cloned.1.call-done = bf16[128,36864]{1,0:T(8,128)(2,1)} async-done(((bf16[8,36864]{1,0:T(8,128)(2,1)}), bf16[128,36864]{1,0:T(8,128)(2,1)}) %all-gather.3.cloned.1.call-update) | async-done | bytes 9437200 | tf_op jit(solution)/shard_map/all_gather | solution.py:74
  119.4 5.1 %convolution_convert_fusion = bf16[32,36864]{1,0:T(8,128)(2,1)S(1)} fusion(bf16[128,36864]{1,0:T(8,128)(2,1)} %all-gather.3.cloned.1.call-done, s32[32]{0:T(128)S(1)} %get-tuple-element.77), kind=kOutput, calls=%fused_computation.26 | convolution fusion | flops 303173632 | bytes 11796608 | tf_op jit(solution)/shard_map/dot_general | solution.py:77
  124.5 4.1 %reshape.152 = bf16[2048,576]{1,0:T(8,128)(2,1)} reshape(bf16[32,36864]{1,0:T(8,128)(2,1)S(1)} %convolution_convert_fusion) | data formatting | bytes 4718592 | tf_op jit(solution)/shard_map/reshape | solution.py:78
  128.6 1.6 slice-done
  130.2 29.5 %while.11 = (s32[]{:T(128)}, bf16[4,512,512]{2,1,0:T(8,128)(2,1)}, s32[4,512]{1,0:T(4,128)S(1)}, bf16[4,512,576]{2,1,0:T(8,128)(2,1)}, bf16[2048,576]{1,0:T(8,12...) while((s32[]{:T(128)}, bf16[4,512,512]{2,1,0:T(8,128)(2,1)}, ...), condition=%wide.region_6.7_spmd.clone, body=%wide.region_3.6_spmd.clone.sunk | while | flops 2296906752 | bytes 18552024 | solution.py:37
  130.4 3.9 %fusion.45 = (f32[512]{0:T(512)S(1)}, f32[512,2048]{1,0:T(8,128)S(1)}) fusion(s32[2048]{0:T(1024)S(1)} %lt.139, s32[512]{0:T(512)S(1)} %bitcast.57, bf16[2048,576]{1,0:T(8,128)(2,1)} %get-tuple-element.145, bf16[4,512,576]{2,1,0:T(8,128)(2,1)} %get-tuple-element.144, s32[]{:T(128)} %get-tuple-element.133), kind=kOutput, calls=%fused_computation.6.clone.1 | convolution fusion | flops 1212153344 | bytes 7483904 | tf_op jit(solution)/shard_map/while/body/eval_jaxpr/dot_general | solution.py:21
  134.3 1.1 fusion.46
  135.4 2.2 %fusion.47 = bf16[4,512,512]{2,1,0:T(8,128)(2,1)} fusion(bf16[4,512,512]{2,1,0:T(8,128)(2,1)} %get-tuple-element.134, s32[]{:T(128)} %get-tuple-element.133, bf16[2048,512]{1,0:T(8,128)(2,1)S(1)} %get-tuple-element.146, f32[512,2048]{1,0:T(8,128)S(1)} %get-tuple-element.123, f32[512]{0:T(512)S(1)} %get-tuple-element.124, s32[2048]{0:T(1024)S(1)} %lt.139, ...), kind=kOutput, calls=%fused_computation.17.clone.1 | convolution fusion | flops 1079508992 | bytes 6830592 | tf_op jit(solution)/shard_map/while/body/eval_jaxpr/dot_general | solution.py:34
  137.8 3.9 %fusion.45 = (f32[512]{0:T(512)S(1)}, f32[512,2048]{1,0:T(8,128)S(1)}) fusion(s32[2048]{0:T(1024)S(1)} %lt.139, s32[512]{0:T(512)S(1)} %bitcast.57, bf16[2048,576]{1,0:T(8,128)(2,1)} %get-tuple-element.145, bf16[4,512,576]{2,1,0:T(8,128)(2,1)} %get-tuple-element.144, s32[]{:T(128)} %get-tuple-element.133), kind=kOutput, calls=%fused_computation.6.clone.1 | convolution fusion | flops 1212153344 | bytes 7483904 | tf_op jit(solution)/shard_map/while/body/eval_jaxpr/dot_general | solution.py:21
  141.7 1.1 fusion.46
  142.8 2.2 %fusion.47 = bf16[4,512,512]{2,1,0:T(8,128)(2,1)} fusion(bf16[4,512,512]{2,1,0:T(8,128)(2,1)} %get-tuple-element.134, s32[]{:T(128)} %get-tuple-element.133, bf16[2048,512]{1,0:T(8,128)(2,1)S(1)} %get-tuple-element.146, f32[512,2048]{1,0:T(8,128)S(1)} %get-tuple-element.123, f32[512]{0:T(512)S(1)} %get-tuple-element.124, s32[2048]{0:T(1024)S(1)} %lt.139, ...), kind=kOutput, calls=%fused_computation.17.clone.1 | convolution fusion | flops 1079508992 | bytes 6830592 | tf_op jit(solution)/shard_map/while/body/eval_jaxpr/dot_general | solution.py:34
  145.1 3.9 %fusion.45 = (f32[512]{0:T(512)S(1)}, f32[512,2048]{1,0:T(8,128)S(1)}) fusion(s32[2048]{0:T(1024)S(1)} %lt.139, s32[512]{0:T(512)S(1)} %bitcast.57, bf16[2048,576]{1,0:T(8,128)(2,1)} %get-tuple-element.145, bf16[4,512,576]{2,1,0:T(8,128)(2,1)} %get-tuple-element.144, s32[]{:T(128)} %get-tuple-element.133), kind=kOutput, calls=%fused_computation.6.clone.1 | convolution fusion | flops 1212153344 | bytes 7483904 | tf_op jit(solution)/shard_map/while/body/eval_jaxpr/dot_general | solution.py:21
  149.1 1.1 fusion.46
  150.2 2.2 %fusion.47 = bf16[4,512,512]{2,1,0:T(8,128)(2,1)} fusion(bf16[4,512,512]{2,1,0:T(8,128)(2,1)} %get-tuple-element.134, s32[]{:T(128)} %get-tuple-element.133, bf16[2048,512]{1,0:T(8,128)(2,1)S(1)} %get-tuple-element.146, f32[512,2048]{1,0:T(8,128)S(1)} %get-tuple-element.123, f32[512]{0:T(512)S(1)} %get-tuple-element.124, s32[2048]{0:T(1024)S(1)} %lt.139, ...), kind=kOutput, calls=%fused_computation.17.clone.1 | convolution fusion | flops 1079508992 | bytes 6830592 | tf_op jit(solution)/shard_map/while/body/eval_jaxpr/dot_general | solution.py:34
  152.5 3.9 %fusion.45 = (f32[512]{0:T(512)S(1)}, f32[512,2048]{1,0:T(8,128)S(1)}) fusion(s32[2048]{0:T(1024)S(1)} %lt.139, s32[512]{0:T(512)S(1)} %bitcast.57, bf16[2048,576]{1,0:T(8,128)(2,1)} %get-tuple-element.145, bf16[4,512,576]{2,1,0:T(8,128)(2,1)} %get-tuple-element.144, s32[]{:T(128)} %get-tuple-element.133), kind=kOutput, calls=%fused_computation.6.clone.1 | convolution fusion | flops 1212153344 | bytes 7483904 | tf_op jit(solution)/shard_map/while/body/eval_jaxpr/dot_general | solution.py:21
  156.4 1.1 fusion.46
  157.6 2.2 %fusion.47 = bf16[4,512,512]{2,1,0:T(8,128)(2,1)} fusion(bf16[4,512,512]{2,1,0:T(8,128)(2,1)} %get-tuple-element.134, s32[]{:T(128)} %get-tuple-element.133, bf16[2048,512]{1,0:T(8,128)(2,1)S(1)} %get-tuple-element.146, f32[512,2048]{1,0:T(8,128)S(1)} %get-tuple-element.123, f32[512]{0:T(512)S(1)} %get-tuple-element.124, s32[2048]{0:T(1024)S(1)} %lt.139, ...), kind=kOutput, calls=%fused_computation.17.clone.1 | convolution fusion | flops 1079508992 | bytes 6830592 | tf_op jit(solution)/shard_map/while/body/eval_jaxpr/dot_general | solution.py:34
  (44 shorter events, 3.3 us)
Async XLA Ops:
  6.5 112.9 %all-gather.3.cloned.1.call-start = ((), (), s32[]{:S(2)}) async-start(), calls=%async_computation | async-start | bytes 10027008 | tf_op jit(solution)/shard_map/all_gather | solution.py:74
  37.3 3.9 %copy-start = (bf16[16,128,576]{1,2,0:T(8,128)(2,1)S(1)}, bf16[16,128,576]{1,2,0:T(8,128)(2,1)}, u32[]{:S(2)}) copy-start(bf16[16,128,576]{1,2,0:T(8,128)(2,1)} %param.6) | copy-start | bytes 7077892
  39.1 4.7 %copy-start.2 = (s32[16]{0:T(128)S(1)}, s32[16]{0:T(128)}, u32[]{:S(2)}) copy-start(s32[16]{0:T(128)} %param.9) | copy-start | bytes 196
  39.1 4.9 %copy-start.1 = (s32[1,32]{1,0:T(1,128)S(1)}, s32[1,32]{1,0:T(1,128)}, u32[]{:S(2)}) copy-start(s32[1,32]{1,0:T(1,128)} %param.8) | copy-start | bytes 388
  128.6 1.6 slice-start
Sparse Core Ops, SparseCore 0:
  41.2 78.1 all-gather.2
where the time goes:
time: 167 us
  waiting for transfers between devices  74.8 us (45%)
  matrix products  29.5 us (18%)
  blocking collectives  23.3 us (14%)
  local copies, waits for them, and re-layouts  17.7 us (11%)
  between operations  13.5 us (8%)
  other arithmetic  7.79 us (5%)
    all_gather x1, waiting for transfers between devices, shards(): portion = lax.all_gather(candidates, 'ctx', axis=0, tiled=True)  74.8 us
    all_gather x1, blocking collectives, shards(): all_picks = lax.all_gather(block_picks, 'ctx', axis=0, tiled=True)  23.3 us
    dot_general x4, matrix products, per_block(): lax.dot_general(block_queries, key_rows, (((1,), (1,)), ((), ())), prefer...  15.7 us
    dot_general x4, matrix products, per_block(): jnp.dot(weights, latent, preferred_element_type=jnp.float32) / normaliser  8.69 us
    dot_general x1, matrix products, shards(): jnp.dot(pick_one, portion, preferred_element_type=jnp.float32)  5.07 us
    reduce_sum x4, other arithmetic, per_block(): normaliser = jnp.sum(exponent, axis=1, keepdims=True)  4.46 us
    unnamed x10, local copies, waits for them, and re-layouts  4.33 us
    reshape x1, local copies, waits for them, and re-layouts, shards(): key_rows = chosen.reshape(TOPK * BLOCK, feature)  4.14 us
  transfers between devices with their start and end apart: 1, of which 1 were waited for; matrix products, arithmetic and copies ran while one was open for 2% of the time, Pallas kernels for 0%

commit v1 on v0

--- a/solution.py
+++ b/solution.py
@@ -54,7 +54,14 @@
     own_picks = block_picks[0]
     owners = own_picks // owned
     union_size = 2 * capacity
-    all_picks = lax.all_gather(block_picks, "ctx", axis=0, tiled=True)
+    size = lax.axis_size("ctx")
+    right = [(i, (i + 1) % size) for i in range(size)]
+    parts = [block_picks]
+    for far in range(1, size):
+        parts = [lax.ppermute(parts[0], "ctx", right), *parts]
+    whole = jnp.concatenate(parts, axis=0)
+    offset = (lax.axis_index("ctx") + 1) * parts[-1].shape[0]
+    all_picks = jnp.roll(whole, offset, axis=0)
     selected_flag = (
         jnp.zeros((ctx_count * owned,), jnp.int32)
         .at[all_picks.reshape(-1)]

time: 167 us -> 233 us (1.40)
  waiting for transfers between devices: 74.8 us -> 157 us
  blocking collectives: 23.3 us -> 0 us
  local copies, waits for them, and re-layouts: 17.7 us -> 23.8 us
    ppermute x0 -> x15, waiting for transfers between devices: none -> 82 us  [shards(): parts = [lax.ppermute(parts[0], 'ctx', right), *parts]]
    all_gather x1 -> x0, blocking collectives: 23.3 us -> none  [shards(): all_picks = lax.all_gather(block_picks, 'ctx', axis=0, tiled=True)]
    concatenate x0 -> x1, local copies, waits for them, and re-layouts: none -> 2.89 us  [shards(): all_picks = jnp.roll(whole, offset, axis=0)]
    unnamed x10 -> x38, local copies, waits for them, and re-layouts: 4.33 us -> 5.46 us
  transfers between devices with their start and end apart: 1 -> 16, of which waited for: 1 -> 16; matrix products, arithmetic and copies ran while one was open for 2% -> 3% of each run, Pallas kernels for 0% -> 0%
where the time goes in v1:
time: 233 us
  waiting for transfers between devices  157 us (67%)
  matrix products  29.5 us (13%)
  local copies, waits for them, and re-layouts  23.8 us (10%)
  between operations  13.6 us (6%)
  other arithmetic  8.45 us (4%)
    ppermute x15, waiting for transfers between devices, shards(): parts = [lax.ppermute(parts[0], 'ctx', right), *parts]  82 us
    all_gather x1, waiting for transfers between devices, shards(): portion = lax.all_gather(candidates, 'ctx', axis=0, tiled=True)  75.2 us
    dot_general x4, matrix products, per_block(): lax.dot_general(block_queries, key_rows, (((1,), (1,)), ((), ())), prefer...  15.7 us
    dot_general x4, matrix products, per_block(): jnp.dot(weights, latent, preferred_element_type=jnp.float32) / normaliser  8.69 us
    unnamed x38, local copies, waits for them, and re-layouts  5.46 us
    dot_general x1, matrix products, shards(): jnp.dot(pick_one, portion, preferred_element_type=jnp.float32)  5.07 us
  transfers between devices with their start and end apart: 16, of which 16 were waited for; matrix products, arithmetic and copies ran while one was open for 3% of the time, Pallas kernels for 0%

profile of v1, /device:TPU:0, one launch (start us, length us, event | category | flops | bytes accessed | tf_op | source)
XLA Modules:
  0.0 233.1 jit_solution(13429192907913369566)
XLA Ops:
  7.0 6.4 %collective-permute-done = s32[1,32]{1,0:T(1,128)S(1)} collective-permute-done((s32[1,32]{1,0:T(1,128)}, s32[1,32]{1,0:T(1,128)S(1)}, u32[]{:S(2)}, u32[]{:S(2)}) %collective-permute-start) | collective-permute-done | bytes 160 | tf_op jit(solution)/shard_map/ppermute | solution.py:61
  14.0 5.7 %collective-permute-done.1 = s32[1,32]{1,0:T(1,128)S(1)} collective-permute-done((s32[1,32]{1,0:T(1,128)S(1)}, s32[1,32]{1,0:T(1,128)S(1)}, u32[]{:S(2)}, u32[]{:S(2)}) %collective-permute-start.1) | collective-permute-done | bytes 160 | tf_op jit(solution)/shard_map/ppermute | solution.py:61
  19.7 5.7 %collective-permute-done.2 = s32[1,32]{1,0:T(1,128)S(1)} collective-permute-done((s32[1,32]{1,0:T(1,128)S(1)}, s32[1,32]{1,0:T(1,128)S(1)}, u32[]{:S(2)}, u32[]{:S(2)}) %collective-permute-start.2) | collective-permute-done | bytes 160 | tf_op jit(solution)/shard_map/ppermute | solution.py:61
  25.4 5.7 %collective-permute-done.3 = s32[1,32]{1,0:T(1,128)S(1)} collective-permute-done((s32[1,32]{1,0:T(1,128)S(1)}, s32[1,32]{1,0:T(1,128)S(1)}, u32[]{:S(2)}, u32[]{:S(2)}) %collective-permute-start.3) | collective-permute-done | bytes 160 | tf_op jit(solution)/shard_map/ppermute | solution.py:61
  31.1 5.7 %collective-permute-done.4 = s32[1,32]{1,0:T(1,128)S(1)} collective-permute-done((s32[1,32]{1,0:T(1,128)S(1)}, s32[1,32]{1,0:T(1,128)S(1)}, u32[]{:S(2)}, u32[]{:S(2)}) %collective-permute-start.4) | collective-permute-done | bytes 160 | tf_op jit(solution)/shard_map/ppermute | solution.py:61
  36.7 5.7 %collective-permute-done.5 = s32[1,32]{1,0:T(1,128)S(1)} collective-permute-done((s32[1,32]{1,0:T(1,128)S(1)}, s32[1,32]{1,0:T(1,128)S(1)}, u32[]{:S(2)}, u32[]{:S(2)}) %collective-permute-start.5) | collective-permute-done | bytes 160 | tf_op jit(solution)/shard_map/ppermute | solution.py:61
  42.4 5.7 %collective-permute-done.6 = s32[1,32]{1,0:T(1,128)S(1)} collective-permute-done((s32[1,32]{1,0:T(1,128)S(1)}, s32[1,32]{1,0:T(1,128)S(1)}, u32[]{:S(2)}, u32[]{:S(2)}) %collective-permute-start.6) | collective-permute-done | bytes 160 | tf_op jit(solution)/shard_map/ppermute | solution.py:61
  48.1 5.7 %collective-permute-done.7 = s32[1,32]{1,0:T(1,128)S(1)} collective-permute-done((s32[1,32]{1,0:T(1,128)S(1)}, s32[1,32]{1,0:T(1,128)S(1)}, u32[]{:S(2)}, u32[]{:S(2)}) %collective-permute-start.7) | collective-permute-done | bytes 160 | tf_op jit(solution)/shard_map/ppermute | solution.py:61
  53.8 5.7 %collective-permute-done.8 = s32[1,32]{1,0:T(1,128)S(1)} collective-permute-done((s32[1,32]{1,0:T(1,128)S(1)}, s32[1,32]{1,0:T(1,128)S(1)}, u32[]{:S(2)}, u32[]{:S(2)}) %collective-permute-start.8) | collective-permute-done | bytes 160 | tf_op jit(solution)/shard_map/ppermute | solution.py:61
  59.5 5.7 %collective-permute-done.9 = s32[1,32]{1,0:T(1,128)S(1)} collective-permute-done((s32[1,32]{1,0:T(1,128)S(1)}, s32[1,32]{1,0:T(1,128)S(1)}, u32[]{:S(2)}, u32[]{:S(2)}) %collective-permute-start.9) | collective-permute-done | bytes 160 | tf_op jit(solution)/shard_map/ppermute | solution.py:61
  65.2 5.7 %collective-permute-done.10 = s32[1,32]{1,0:T(1,128)S(1)} collective-permute-done((s32[1,32]{1,0:T(1,128)S(1)}, s32[1,32]{1,0:T(1,128)S(1)}, u32[]{:S(2)}, u32[]{:S(2)}) %collective-permute-start.10) | collective-permute-done | bytes 160 | tf_op jit(solution)/shard_map/ppermute | solution.py:61
  70.9 5.7 %collective-permute-done.11 = s32[1,32]{1,0:T(1,128)S(1)} collective-permute-done((s32[1,32]{1,0:T(1,128)S(1)}, s32[1,32]{1,0:T(1,128)S(1)}, u32[]{:S(2)}, u32[]{:S(2)}) %collective-permute-start.11) | collective-permute-done | bytes 160 | tf_op jit(solution)/shard_map/ppermute | solution.py:61
  76.6 5.7 %collective-permute-done.12 = s32[1,32]{1,0:T(1,128)S(1)} collective-permute-done((s32[1,32]{1,0:T(1,128)S(1)}, s32[1,32]{1,0:T(1,128)S(1)}, u32[]{:S(2)}, u32[]{:S(2)}) %collective-permute-start.12) | collective-permute-done | bytes 160 | tf_op jit(solution)/shard_map/ppermute | solution.py:61
  88.5 5.1 %collective-permute-done.14 = s32[1,32]{1,0:T(1,128)} collective-permute-done((s32[1,32]{1,0:T(1,128)S(1)}, s32[1,32]{1,0:T(1,128)}, u32[]{:S(2)}, u32[]{:S(2)}) %collective-permute-start.14) | collective-permute-done | bytes 160 | tf_op jit(solution)/shard_map/ppermute | solution.py:61
  93.6 2.9 %concatenate.6 = s32[32,32]{1,0:T(8,128)S(1)} concatenate(s32[1,32]{1,0:T(1,128)} %collective-permute-done.14, s32[1,32]{1,0:T(1,128)} %copy-done.15, s32[1,32]{1,0:T(1,128)} %copy-done.14, s32[1,32]{1,0:T(1,128)} %copy-done.13, s32[1,32]{1,0:T(1,128)} %copy-done.12, s32[1,32]{1,0:T(1,128)} %copy-done.11, s32[1,32]{1,0:T(1,128)} %copy-done.10, s32[1,32]{1,0:T(1,128)} %copy-done.9, ...), dimensions={0} | concatenate | bytes 8192 | tf_op jit(solution)/shard_map/jit(_roll_dynamic)/concatenate | solution.py:64
  97.9 3.0 %scatter_custom_fusion = s32[256]{0:T(256)} fusion(s32[512]{0:T(512)S(1)} %bitcast.60, s32[512]{0:T(512)S(1)} %broadcast.155, s32[]{:T(128)} %copy.22), kind=kCustom, calls=%fused_computation.59 | custom fusion | bytes 1028 | tf_op jit(solution)/shard_map/scatter | solution.py:68
  110.7 75.2 %all-gather.2.cloned.1.call-done = bf16[128,36864]{1,0:T(8,128)(2,1)} async-done(((bf16[8,36864]{1,0:T(8,128)(2,1)}), bf16[128,36864]{1,0:T(8,128)(2,1)}) %all-gather.2.cloned.1.call-update) | async-done | bytes 9437200 | tf_op jit(solution)/shard_map/all_gather | solution.py:81
  185.9 5.1 %convolution_convert_fusion = bf16[32,36864]{1,0:T(8,128)(2,1)S(1)} fusion(bf16[128,36864]{1,0:T(8,128)(2,1)} %all-gather.2.cloned.1.call-done, s32[32]{0:T(128)S(1)} %get-tuple-element.77), kind=kOutput, calls=%fused_computation.26 | convolution fusion | flops 303173632 | bytes 11796608 | tf_op jit(solution)/shard_map/dot_general | solution.py:84
  191.0 4.2 %reshape.152 = bf16[2048,576]{1,0:T(8,128)(2,1)} reshape(bf16[32,36864]{1,0:T(8,128)(2,1)S(1)} %convolution_convert_fusion) | data formatting | bytes 4718592 | tf_op jit(solution)/shard_map/reshape | solution.py:85
  196.7 29.5 %while.11 = (s32[]{:T(128)}, bf16[4,512,512]{2,1,0:T(8,128)(2,1)}, s32[4,512]{1,0:T(4,128)S(1)}, bf16[4,512,576]{2,1,0:T(8,128)(2,1)}, bf16[2048,576]{1,0:T(8,12...) while((s32[]{:T(128)}, bf16[4,512,512]{2,1,0:T(8,128)(2,1)}, ...), condition=%wide.region_6.7_spmd.clone, body=%wide.region_3.6_spmd.clone.sunk | while | flops 2296906752 | bytes 18552024 | solution.py:37
  196.9 3.9 %fusion.46 = (f32[512]{0:T(512)S(1)}, f32[512,2048]{1,0:T(8,128)S(1)}) fusion(s32[2048]{0:T(1024)S(1)} %lt.153, s32[512]{0:T(512)S(1)} %bitcast.56, bf16[2048,576]{1,0:T(8,128)(2,1)} %get-tuple-element.145, bf16[4,512,576]{2,1,0:T(8,128)(2,1)} %get-tuple-element.144, s32[]{:T(128)} %get-tuple-element.133), kind=kOutput, calls=%fused_computation.6.clone.1 | convolution fusion | flops 1212153344 | bytes 7483904 | tf_op jit(solution)/shard_map/while/body/eval_jaxpr/dot_general | solution.py:21
  204.2 3.9 %fusion.46 = (f32[512]{0:T(512)S(1)}, f32[512,2048]{1,0:T(8,128)S(1)}) fusion(s32[2048]{0:T(1024)S(1)} %lt.153, s32[512]{0:T(512)S(1)} %bitcast.56, bf16[2048,576]{1,0:T(8,128)(2,1)} %get-tuple-element.145, bf16[4,512,576]{2,1,0:T(8,128)(2,1)} %get-tuple-element.144, s32[]{:T(128)} %get-tuple-element.133), kind=kOutput, calls=%fused_computation.6.clone.1 | convolution fusion | flops 1212153344 | bytes 7483904 | tf_op jit(solution)/shard_map/while/body/eval_jaxpr/dot_general | solution.py:21
  211.6 3.9 %fusion.46 = (f32[512]{0:T(512)S(1)}, f32[512,2048]{1,0:T(8,128)S(1)}) fusion(s32[2048]{0:T(1024)S(1)} %lt.153, s32[512]{0:T(512)S(1)} %bitcast.56, bf16[2048,576]{1,0:T(8,128)(2,1)} %get-tuple-element.145, bf16[4,512,576]{2,1,0:T(8,128)(2,1)} %get-tuple-element.144, s32[]{:T(128)} %get-tuple-element.133), kind=kOutput, calls=%fused_computation.6.clone.1 | convolution fusion | flops 1212153344 | bytes 7483904 | tf_op jit(solution)/shard_map/while/body/eval_jaxpr/dot_general | solution.py:21
  219.0 3.9 %fusion.46 = (f32[512]{0:T(512)S(1)}, f32[512,2048]{1,0:T(8,128)S(1)}) fusion(s32[2048]{0:T(1024)S(1)} %lt.153, s32[512]{0:T(512)S(1)} %bitcast.56, bf16[2048,576]{1,0:T(8,128)(2,1)} %get-tuple-element.145, bf16[4,512,576]{2,1,0:T(8,128)(2,1)} %get-tuple-element.144, s32[]{:T(128)} %get-tuple-element.133), kind=kOutput, calls=%fused_computation.6.clone.1 | convolution fusion | flops 1212153344 | bytes 7483904 | tf_op jit(solution)/shard_map/while/body/eval_jaxpr/dot_general | solution.py:21
  (101 shorter events, 33.7 us)
Async XLA Ops:
  6.5 179.3 %all-gather.2.cloned.1.call-start = ((), (), s32[]{:S(2)}) async-start(), calls=%async_computation | async-start | bytes 10027008 | tf_op jit(solution)/shard_map/all_gather | solution.py:81
  6.5 6.9 %collective-permute-start = (s32[1,32]{1,0:T(1,128)}, s32[1,32]{1,0:T(1,128)S(1)}, u32[]{:S(2)}, u32[]{:S(2)}) collective-permute-start(s32[1,32]{1,0:T(1,128)} %param.8), channel_id=1, source_target_pairs={{0,1},{1,2},{2,3},{3,4},{4,5},{5,6},{6,7},{7,8},{8,9},{9,10},{10,1... | collective-permute-start | bytes 392 | tf_op jit(solution)/shard_map/ppermute | solution.py:61
  14.0 5.7 %collective-permute-start.1 = (s32[1,32]{1,0:T(1,128)S(1)}, s32[1,32]{1,0:T(1,128)S(1)}, u32[]{:S(2)}, u32[]{:S(2)}) collective-permute-start(s32[1,32]{1,0:T(1,128)S(1)} %collective-permute-done), channel_id=1, source_target_pairs={{0,1},{1,2},{2,3},{3,4},{4,5},{5,6},{6,7},{7,8},{8,9},{9,10},{10,1... | collective-permute-start | bytes 392 | tf_op jit(solution)/shard_map/ppermute | solution.py:61
  19.7 62.6 %copy-start.3 = (s32[1,32]{1,0:T(1,128)}, s32[1,32]{1,0:T(1,128)S(1)}, u32[]{:S(2)}) copy-start(s32[1,32]{1,0:T(1,128)S(1)} %collective-permute-done.1) | copy-start | bytes 388
  19.7 5.7 %collective-permute-start.2 = (s32[1,32]{1,0:T(1,128)S(1)}, s32[1,32]{1,0:T(1,128)S(1)}, u32[]{:S(2)}, u32[]{:S(2)}) collective-permute-start(s32[1,32]{1,0:T(1,128)S(1)} %collective-permute-done.1), channel_id=1, source_target_pairs={{0,1},{1,2},{2,3},{3,4},{4,5},{5,6},{6,7},{7,8},{8,9},{9,10},{10,1... | collective-permute-start | bytes 392 | tf_op jit(solution)/shard_map/ppermute | solution.py:61
  25.4 56.9 %copy-start.4 = (s32[1,32]{1,0:T(1,128)}, s32[1,32]{1,0:T(1,128)S(1)}, u32[]{:S(2)}) copy-start(s32[1,32]{1,0:T(1,128)S(1)} %collective-permute-done.2) | copy-start | bytes 388
  25.4 5.7 %collective-permute-start.3 = (s32[1,32]{1,0:T(1,128)S(1)}, s32[1,32]{1,0:T(1,128)S(1)}, u32[]{:S(2)}, u32[]{:S(2)}) collective-permute-start(s32[1,32]{1,0:T(1,128)S(1)} %collective-permute-done.2), channel_id=1, source_target_pairs={{0,1},{1,2},{2,3},{3,4},{4,5},{5,6},{6,7},{7,8},{8,9},{9,10},{10,1... | collective-permute-start | bytes 392 | tf_op jit(solution)/shard_map/ppermute | solution.py:61
  31.0 51.3 %copy-start.5 = (s32[1,32]{1,0:T(1,128)}, s32[1,32]{1,0:T(1,128)S(1)}, u32[]{:S(2)}) copy-start(s32[1,32]{1,0:T(1,128)S(1)} %collective-permute-done.3) | copy-start | bytes 388
  31.1 5.7 %collective-permute-start.4 = (s32[1,32]{1,0:T(1,128)S(1)}, s32[1,32]{1,0:T(1,128)S(1)}, u32[]{:S(2)}, u32[]{:S(2)}) collective-permute-start(s32[1,32]{1,0:T(1,128)S(1)} %collective-permute-done.3), channel_id=1, source_target_pairs={{0,1},{1,2},{2,3},{3,4},{4,5},{5,6},{6,7},{7,8},{8,9},{9,10},{10,1... | collective-permute-start | bytes 392 | tf_op jit(solution)/shard_map/ppermute | solution.py:61
  36.7 45.6 %copy-start.6 = (s32[1,32]{1,0:T(1,128)}, s32[1,32]{1,0:T(1,128)S(1)}, u32[]{:S(2)}) copy-start(s32[1,32]{1,0:T(1,128)S(1)} %collective-permute-done.4) | copy-start | bytes 388
  36.7 5.7 %collective-permute-start.5 = (s32[1,32]{1,0:T(1,128)S(1)}, s32[1,32]{1,0:T(1,128)S(1)}, u32[]{:S(2)}, u32[]{:S(2)}) collective-permute-start(s32[1,32]{1,0:T(1,128)S(1)} %collective-permute-done.4), channel_id=1, source_target_pairs={{0,1},{1,2},{2,3},{3,4},{4,5},{5,6},{6,7},{7,8},{8,9},{9,10},{10,1... | collective-permute-start | bytes 392 | tf_op jit(solution)/shard_map/ppermute | solution.py:61
  42.4 39.9 %copy-start.7 = (s32[1,32]{1,0:T(1,128)}, s32[1,32]{1,0:T(1,128)S(1)}, u32[]{:S(2)}) copy-start(s32[1,32]{1,0:T(1,128)S(1)} %collective-permute-done.5) | copy-start | bytes 388
  42.4 5.7 %collective-permute-start.6 = (s32[1,32]{1,0:T(1,128)S(1)}, s32[1,32]{1,0:T(1,128)S(1)}, u32[]{:S(2)}, u32[]{:S(2)}) collective-permute-start(s32[1,32]{1,0:T(1,128)S(1)} %collective-permute-done.5), channel_id=1, source_target_pairs={{0,1},{1,2},{2,3},{3,4},{4,5},{5,6},{6,7},{7,8},{8,9},{9,10},{10,1... | collective-permute-start | bytes 392 | tf_op jit(solution)/shard_map/ppermute | solution.py:61
  48.1 34.2 %copy-start.8 = (s32[1,32]{1,0:T(1,128)}, s32[1,32]{1,0:T(1,128)S(1)}, u32[]{:S(2)}) copy-start(s32[1,32]{1,0:T(1,128)S(1)} %collective-permute-done.6) | copy-start | bytes 388
  48.1 5.7 %collective-permute-start.7 = (s32[1,32]{1,0:T(1,128)S(1)}, s32[1,32]{1,0:T(1,128)S(1)}, u32[]{:S(2)}, u32[]{:S(2)}) collective-permute-start(s32[1,32]{1,0:T(1,128)S(1)} %collective-permute-done.6), channel_id=1, source_target_pairs={{0,1},{1,2},{2,3},{3,4},{4,5},{5,6},{6,7},{7,8},{8,9},{9,10},{10,1... | collective-permute-start | bytes 392 | tf_op jit(solution)/shard_map/ppermute | solution.py:61
  53.8 28.5 %copy-start.9 = (s32[1,32]{1,0:T(1,128)}, s32[1,32]{1,0:T(1,128)S(1)}, u32[]{:S(2)}) copy-start(s32[1,32]{1,0:T(1,128)S(1)} %collective-permute-done.7) | copy-start | bytes 388
  53.8 5.7 %collective-permute-start.8 = (s32[1,32]{1,0:T(1,128)S(1)}, s32[1,32]{1,0:T(1,128)S(1)}, u32[]{:S(2)}, u32[]{:S(2)}) collective-permute-start(s32[1,32]{1,0:T(1,128)S(1)} %collective-permute-done.7), channel_id=1, source_target_pairs={{0,1},{1,2},{2,3},{3,4},{4,5},{5,6},{6,7},{7,8},{8,9},{9,10},{10,1... | collective-permute-start | bytes 392 | tf_op jit(solution)/shard_map/ppermute | solution.py:61
  59.5 22.8 %copy-start.10 = (s32[1,32]{1,0:T(1,128)}, s32[1,32]{1,0:T(1,128)S(1)}, u32[]{:S(2)}) copy-start(s32[1,32]{1,0:T(1,128)S(1)} %collective-permute-done.8) | copy-start | bytes 388
  59.5 5.7 %collective-permute-start.9 = (s32[1,32]{1,0:T(1,128)S(1)}, s32[1,32]{1,0:T(1,128)S(1)}, u32[]{:S(2)}, u32[]{:S(2)}) collective-permute-start(s32[1,32]{1,0:T(1,128)S(1)} %collective-permute-done.8), channel_id=1, source_target_pairs={{0,1},{1,2},{2,3},{3,4},{4,5},{5,6},{6,7},{7,8},{8,9},{9,10},{10,1... | collective-permute-start | bytes 392 | tf_op jit(solution)/shard_map/ppermute | solution.py:61
  65.2 5.7 %collective-permute-start.10 = (s32[1,32]{1,0:T(1,128)S(1)}, s32[1,32]{1,0:T(1,128)S(1)}, u32[]{:S(2)}, u32[]{:S(2)}) collective-permute-start(s32[1,32]{1,0:T(1,128)S(1)} %collective-permute-done.9), channel_id=1, source_target_pairs={{0,1},{1,2},{2,3},{3,4},{4,5},{5,6},{6,7},{7,8},{8,9},{9,10},{10,1... | collective-permute-start | bytes 392 | tf_op jit(solution)/shard_map/ppermute | solution.py:61
  70.9 5.7 %collective-permute-start.11 = (s32[1,32]{1,0:T(1,128)S(1)}, s32[1,32]{1,0:T(1,128)S(1)}, u32[]{:S(2)}, u32[]{:S(2)}) collective-permute-start(s32[1,32]{1,0:T(1,128)S(1)} %collective-permute-done.10), channel_id=1, source_target_pairs={{0,1},{1,2},{2,3},{3,4},{4,5},{5,6},{6,7},{7,8},{8,9},{9,10},{10,1... | collective-permute-start | bytes 392 | tf_op jit(solution)/shard_map/ppermute | solution.py:61
  76.6 5.7 %collective-permute-start.12 = (s32[1,32]{1,0:T(1,128)S(1)}, s32[1,32]{1,0:T(1,128)S(1)}, u32[]{:S(2)}, u32[]{:S(2)}) collective-permute-start(s32[1,32]{1,0:T(1,128)S(1)} %collective-permute-done.11), channel_id=1, source_target_pairs={{0,1},{1,2},{2,3},{3,4},{4,5},{5,6},{6,7},{7,8},{8,9},{9,10},{10,1... | collective-permute-start | bytes 392 | tf_op jit(solution)/shard_map/ppermute | solution.py:61
  82.3 5.7 %collective-permute-start.13 = (s32[1,32]{1,0:T(1,128)S(1)}, s32[1,32]{1,0:T(1,128)S(1)}, u32[]{:S(2)}, u32[]{:S(2)}) collective-permute-start(s32[1,32]{1,0:T(1,128)S(1)} %collective-permute-done.12), channel_id=1, source_target_pairs={{0,1},{1,2},{2,3},{3,4},{4,5},{5,6},{6,7},{7,8},{8,9},{9,10},{10,1... | collective-permute-start | bytes 392 | tf_op jit(solution)/shard_map/ppermute | solution.py:61
  88.0 5.6 %collective-permute-start.14 = (s32[1,32]{1,0:T(1,128)S(1)}, s32[1,32]{1,0:T(1,128)}, u32[]{:S(2)}, u32[]{:S(2)}) collective-permute-start(s32[1,32]{1,0:T(1,128)S(1)} %collective-permute-done.13), channel_id=1, source_target_pairs={{0,1},{1,2},{2,3},{3,4},{4,5},{5,6},{6,7},{7,8},{8,9},{9,10},{10,1... | collective-permute-start | bytes 392 | tf_op jit(solution)/shard_map/ppermute | solution.py:61
  (10 other events, 73.7 us)
Sparse Core Ops, SparseCore 0:
  107.3 78.5 all-gather.1
